TPU v7x, 32 devices: a whole 2x2x4 slice. The times are simulated.
32 devices in a mesh: groups: 2 (over y), ep: 4 (over x, core), tp: 4 (over z).
Axes of the slice: x: 2, y: 2, z: 4, core: 2. Of those that a mesh axis runs over, the one named last changes fastest.
Arguments:
- hidden_in: bfloat16 [32, 4, 3584], P(('groups', 'ep', 'tp')), parts along dimension 0, may hold values from -12 to 12
- queries: bfloat16 [32, 4, 128, 576], P(('groups', 'ep', 'tp')), parts along dimension 0, may hold values from -100 to 100
- kv_cache: bfloat16 [32, 2048, 576], P(('groups', 'ep', 'tp')), parts along dimension 0, may hold values from -6 to 6
- new_kv: bfloat16 [32, 4, 576], P(('groups', 'ep', 'tp')), parts along dimension 0, may hold values from -8 to 8
- lengths: int32 [32], P(('groups', 'ep', 'tp')), parts along dimension 0, may hold values from 128 to 2048, as said below
- expert_ids: int32 [32, 4, 2], P(('groups', 'ep')), parts along dimension 0, may hold values from 0 to 3, all different within a row; in each aligned block of 16 rows (0 to 15, 16 to 31, ..., all dimensions but the last counted through in order) at most 12 rows name the same one
- value_up: bfloat16 [128, 512, 128], P(('ep', 'tp')), may hold values from -3 to 3
- out_proj: bfloat16 [128, 128, 3584], P(('ep', 'tp')), may hold values from -0.046875 to 0.046875
- norm_gain: bfloat16 [3584], replicated, may hold values from 0.099609375 to 1.8984375
- router: bfloat16 [3584, 4], replicated, may hold values from -0.09375 to 0.09375
- expert_in: bfloat16 [4, 2, 3584, 2048], P('ep', None, None, 'tp'), may hold values from -0.09375 to 0.09375
- expert_out: bfloat16 [4, 2048, 3584], P('ep', 'tp'), may hold values from -0.125 to 0.125
- shared_in: bfloat16 [2, 3584, 1024], P(None, None, 'tp'), may hold values from -0.09375 to 0.09375
- shared_out: bfloat16 [1024, 3584], P('tp'), may hold values from -0.1875 to 0.1875
Outputs:
- layer_out: bfloat16 [32, 4, 3584], P(('groups', 'ep', 'tp')), parts along dimension 0
There are 2 independent parts, one for each index of `groups`. A program takes and returns all parts, laid end to end along the dimension named above; an argument that names none is the same for every part. Nothing has to cross between parts.
Inputs may be any that keep to these rules, and one draw needn't show every extreme that they name: `expert_ids`: each row and step names 2 distinct experts; within the rows of one index of ep, over all 4 steps, no expert is named more than 12 times, and in every draw some expert is named exactly 12 times there. `lengths`: some row uses all 2048 cached positions.
All inputs are finite; a program needn't handle non-finite values.
Results may differ from a plain program's by a relative error of at most 0.014.
Values may be sent and summed in bfloat16 or wider, within the bound.
No kernel may reach another device: no remote copies, remote signals or barrier semaphores. Data moves between devices by JAX's collectives and lax.ppermute only.
A program may use at most 64 MiB of HBM per device.

v0:
```python
import jax
import jax.numpy as jnp
from jax import lax
from jax.sharding import PartitionSpec as P

LAT = 512
score_scale = 192.0 ** (-0.5)
route_scale = 2.5
norm_eps = 1e-06


def attend_block(queries, kv_cache, new_kv, lengths):
    rows_here, steps_here, heads_here, kv_width = queries.shape
    positions = kv_cache.shape[1]
    cached = (
        jnp.einsum("rshk,rck->rshc", queries, kv_cache, preferred_element_type=jnp.float32)
        * score_scale
    )
    recent = (
        jnp.einsum("rshk,rjk->rshj", queries, new_kv, preferred_element_type=jnp.float32)
        * score_scale
    )
    cache_live = lax.broadcasted_iota(jnp.int32, (rows_here, positions), 1) < lengths[:, None]
    causal = lax.broadcasted_iota(jnp.int32, (steps_here, steps_here), 1) <= lax.broadcasted_iota(
        jnp.int32, (steps_here, steps_here), 0
    )
    cached = jnp.where(cache_live[:, None, None, :], cached, -1e30)
    recent = jnp.where(causal[None, :, None, :], recent, -1e30)
    highest = jnp.maximum(cached.max(-1), recent.max(-1))[..., None]
    cached_exp = jnp.exp(cached - highest)
    recent_exp = jnp.exp(recent - highest)
    denominator = cached_exp.sum(-1, keepdims=True) + recent_exp.sum(-1, keepdims=True)
    cached_prob = (cached_exp / denominator).astype(jnp.bfloat16)
    recent_prob = (recent_exp / denominator).astype(jnp.bfloat16)
    combined = jnp.einsum(
        "rshc,rck->rshk", cached_prob, kv_cache, preferred_element_type=jnp.float32
    )
    combined = combined + jnp.einsum(
        "rshj,rjk->rshk", recent_prob, new_kv, preferred_element_type=jnp.float32
    )
    return combined[..., :LAT].astype(jnp.bfloat16)


def on_device(
    hidden_in,
    queries,
    kv_cache,
    new_kv,
    lengths,
    expert_ids,
    value_up,
    out_proj,
    norm_gain,
    router,
    expert_in,
    expert_out,
    shared_in,
    shared_out,
):
    rows_here = hidden_in.shape[0]
    steps_here = hidden_in.shape[1]
    model_width = hidden_in.shape[2]
    latent_out = attend_block(queries, kv_cache, new_kv, lengths)
    by_head = lax.all_to_all(latent_out, ("ep", "tp"), split_axis=2, concat_axis=0, tiled=True)
    head_vals = jnp.einsum(
        "rshl,hlv->rshv", by_head, value_up, preferred_element_type=jnp.float32
    ).astype(jnp.bfloat16)
    attention = lax.psum_scatter(
        jnp.einsum("rshv,hvd->rsd", head_vals, out_proj, preferred_element_type=jnp.float32),
        ("ep", "tp"),
        scatter_dimension=0,
        tiled=True,
    )
    residual = hidden_in.astype(jnp.float32) + attention
    mean_square = jnp.mean(residual * residual, axis=-1, keepdims=True)
    normed = (residual * lax.rsqrt(mean_square + norm_eps) * norm_gain.astype(jnp.float32)).astype(
        jnp.bfloat16
    )
    block_items = lax.all_gather(
        normed.reshape(rows_here * steps_here, model_width), "tp", axis=0, tiled=True
    )
    item_count = block_items.shape[0]
    expert_count = router.shape[1]
    capacity = 3 * item_count // 4
    affinity = jax.nn.sigmoid(jnp.dot(block_items, router, preferred_element_type=jnp.float32))
    picked = expert_ids.reshape(item_count, expert_ids.shape[2])
    expert_iota = lax.broadcasted_iota(jnp.int32, (1, 1, expert_count), 2)
    chosen = jnp.sum((picked[:, :, None] == expert_iota).astype(jnp.int32), axis=1)
    scored = chosen.astype(jnp.float32) * affinity
    gate_weight = route_scale * scored / jnp.sum(scored, axis=-1, keepdims=True)
    slot_index = jnp.cumsum(chosen, axis=0) - chosen
    slot_iota = lax.broadcasted_iota(jnp.int32, (1, 1, capacity), 2)
    slot_hit = (slot_index[:, :, None] == slot_iota) & (chosen[:, :, None] > 0)
    outgoing = jnp.einsum(
        "mux,mt->uxt",
        slot_hit.astype(jnp.bfloat16),
        block_items,
        preferred_element_type=jnp.float32,
    ).astype(jnp.bfloat16)
    arrived = lax.all_to_all(outgoing, "ep", split_axis=0, concat_axis=0, tiled=True)
    gate_part = jnp.einsum(
        "scd,df->scf", arrived, expert_in[0, 0], preferred_element_type=jnp.float32
    )
    up_part = jnp.einsum(
        "scd,df->scf", arrived, expert_in[0, 1], preferred_element_type=jnp.float32
    )
    activated = (jax.nn.silu(gate_part) * up_part).astype(jnp.bfloat16)
    produced = jnp.einsum(
        "scf,fd->scd", activated, expert_out[0], preferred_element_type=jnp.float32
    )
    returned_slots = lax.all_to_all(
        produced.astype(jnp.bfloat16), "ep", split_axis=0, concat_axis=0, tiled=True
    ).astype(produced.dtype)
    combine = jnp.where(slot_hit, gate_weight[:, :, None], 0.0)
    routed_part = jnp.einsum(
        "jpo,pos->js",
        combine,
        returned_slots,
        precision=lax.Precision.HIGHEST,
        preferred_element_type=jnp.float32,
    )
    shared_gate = jnp.dot(block_items, shared_in[0], preferred_element_type=jnp.float32)
    shared_up = jnp.dot(block_items, shared_in[1], preferred_element_type=jnp.float32)
    shared_act = (jax.nn.silu(shared_gate) * shared_up).astype(jnp.bfloat16)
    shared_part = jnp.dot(shared_act, shared_out, preferred_element_type=jnp.float32)
    expert_sum = lax.psum_scatter(
        (routed_part + shared_part).astype(jnp.bfloat16), "tp", scatter_dimension=0, tiled=True
    ).astype(jnp.float32)
    layer_out = (residual + expert_sum.reshape(rows_here, steps_here, model_width)).astype(
        jnp.bfloat16
    )
    return layer_out


def solution(mesh):
    in_specs = (
        P(("groups", "ep", "tp"), None, None),
        P(("groups", "ep", "tp"), None, None, None),
        P(("groups", "ep", "tp"), None, None),
        P(("groups", "ep", "tp"), None, None),
        P(("groups", "ep", "tp")),
        P(("groups", "ep"), None, None),
        P(("ep", "tp"), None, None),
        P(("ep", "tp"), None, None),
        P(),
        P(),
        P("ep", None, None, "tp"),
        P("ep", "tp", None),
        P(None, None, "tp"),
        P("tp", None),
    )
    out_specs = P(("groups", "ep", "tp"), None, None)
    return jax.shard_map(
        on_device, mesh=mesh, in_specs=in_specs, out_specs=out_specs, check_vma=False
    )
```

profile of v0, /device:TPU:0, one launch (start us, length us, event | category | flops | bytes accessed | tf_op | source)
XLA Modules:
  0.0 234.1 jit_solution(7596553311977979096)
XLA Ops:
  6.5 0.0 copy-start
  6.5 0.0 copy-start.1
  6.5 0.0 all-reduce.5.cloned.1.call-start
  7.4 0.8 copy-done
  8.2 3.2 %fusion.6 = (f32[4,128]{1,0:T(4,128)S(1)}, f32[4,128,2048]{2,1,0:T(8,128)S(1)}) fusion(pred[2048]{0:T(1024)(128)(4,1)S(1)} %iota_compare_fusion.1, bf16[1,2048,576]{1,2,0:T(8,128)(2,1)S(1)} %copy-done, bf16[1,4,128,576]{2,3,1,0:T(8,128)(2,1)} %param.15), kind=kOutput, calls=%fused_computation.11 | convolution fusion | flops 1211104768 | bytes 7147520 | tf_op jit(solution)/shard_map/rshk,rck->rshc/dot_general | solution.py:16
  11.4 0.0 copy-done.1
  11.4 0.0 copy-done.3
  11.4 0.2 fusion.97
  11.6 0.9 fusion.14
  12.6 1.7 fusion.15
  14.3 0.4 fusion.27
  14.7 0.4 copy.40
  15.1 22.8 %all_to_all.28 = bf16[1,4,128,512]{3,1,0,2:T(4,128)(2,1)} all-to-all(bf16[1,4,128,512]{3,1,0,2:T(4,128)(2,1)S(1)} %copy.40), channel_id=1, replica_groups=mesh['groups'=2,'ep'=4,'tp'=4] {'ep','tp'}, dimensions={2} | all-to-all | bytes 1048576 | tf_op jit(solution)/shard_map/all_to_all | solution.py:64
  38.0 5.3 %fusion.2 = f32[16,4,3584]{2,0,1:T(8,128)S(1)} fusion(bf16[8,128,3584]{2,1,0:T(8,128)(2,1)} %param.21, bf16[8,512,128]{2,1,0:T(8,128)(2,1)} %param.20, bf16[1,4,16,8,512]{4,1,3,2,0:T(4,128)(2,1)} %bitcast.112), kind=kOutput, calls=%fused_computation.2 | convolution fusion | flops 536936448 | bytes 9830400 | tf_op jit(solution)/shard_map/rshv,hvd->rsd/dot_general | solution.py:69
  43.3 0.0 copy-start.6
  43.3 1.6 copy.43
  44.9 0.0 all-reduce.5.cloned.1.call-update
  44.9 0.0 copy-done.4
  44.9 0.0 copy-done.5
  44.9 0.1 eq.28
  45.0 0.1 copy.45
  45.2 0.1 copy.47
  45.3 0.0 copy-done.8
  45.3 0.6 dynamic-slice
  45.9 90.4 %all-reduce.5.cloned.1.call-done = f32[16,4,3584]{2,1,0:T(4,128)} async-done(((f32[16,4,3584]{2,1,0:T(4,128)}), f32[16,4,3584]{2,1,0:T(4,128)}) %all-reduce.5.cloned.1.call-update) | async-done | bytes 917520
  136.2 0.0 copy-done.2
  136.2 1.5 multiply_reduce_fusion
  137.8 1.5 multiply_convert_fusion
  139.3 14.3 %all-gather = bf16[1,16,3584]{2,0,1:T(2,128)(2,1)S(1)} all-gather(bf16[1,4,3584]{2,0,1:T(2,128)(2,1)S(1)} %copy.48), channel_id=2, replica_groups=mesh['groups'=2,'ep'=4,'tp'=4] {'tp'}, dimensions={1}, use_global_device_ids=true | all-gather | bytes 143360 | tf_op jit(solution)/shard_map/all_gather | solution.py:79
  153.7 1.2 convolution_convert_fusion.1
  154.8 3.5 %all-to-all-start.1 = ((bf16[4,12,3584]{2,1,0:T(8,128)(2,1)}), bf16[4,12,3584]{2,1,0:T(8,128)(2,1)S(1)}, u32[]{:S(2)}, u32[]{:S(2)}) async-start(bf16[4,12,3584]{2,1,0:T(8,128)(2,1)} %convolution_convert_fusion.1), calls=%async_computation.1 | async-start | bytes 917504 | tf_op jit(solution)/shard_map/all_to_all | solution.py:100
  158.3 0.0 copy-done.6
  158.3 0.2 fusion.98
  158.5 7.9 %all-to-all-done.1 = bf16[4,12,3584]{2,1,0:T(8,128)(2,1)S(1)} async-done(((bf16[4,12,3584]{2,1,0:T(8,128)(2,1)}), bf16[4,12,3584]{2,1,0:T(8,128)(2,1)S(1)}, u32[]{:S(2)}, u32[]{:S(2)}) %all-to-all-start.1) | async-done | bytes 344096 | tf_op jit(solution)/shard_map/all_to_all | solution.py:100
  166.4 2.8 %fusion.9 = f32[4,12,512]{2,1,0:T(8,128)S(1)} fusion(bf16[4,12,3584]{2,1,0:T(8,128)(2,1)S(1)} %all-to-all-done.1, bf16[1,2,3584,512]{3,2,1,0:T(8,128)(2,1)} %param.24), kind=kOutput, calls=%fused_computation.14 | convolution fusion | flops 176160768 | bytes 4112384 | tf_op jit(solution)/shard_map/scd,df->scf/dot_general | solution.py:101
  169.2 5.4 %convolution_convert_fusion = bf16[4,12,3584]{2,1,0:T(8,128)(2,1)} fusion(bf16[1,512,3584]{2,1,0:T(8,128)(2,1)} %param.25, bf16[4,12,3584]{2,1,0:T(8,128)(2,1)S(1)} %all-to-all-done.1, bf16[1,2,3584,512]{3,2,1,0:T(8,128)(2,1)} %param.24, f32[4,12,512]{2,1,0:T(8,128)S(1)} %fusion.9), kind=kOutput, calls=%fused_computation.3 | convolution fusion | flops 352641024 | bytes 8126464 | tf_op jit(solution)/shard_map/scf,fd->scd/dot_general | solution.py:108
  174.6 3.5 %all-to-all-start.2 = ((bf16[4,12,3584]{2,1,0:T(8,128)(2,1)}), bf16[4,12,3584]{2,1,0:T(8,128)(2,1)S(1)}, u32[]{:S(2)}, u32[]{:S(2)}) async-start(bf16[4,12,3584]{2,1,0:T(8,128)(2,1)} %convolution_convert_fusion), calls=%async_computation.2 | async-start | bytes 917504 | tf_op jit(solution)/shard_map/all_to_all | solution.py:111
  178.0 0.0 copy-start.7
  178.1 0.0 all-reduce.7.cloned.1.call-start
  178.1 1.8 fusion.22
  180.0 6.2 %all-to-all-done.2 = bf16[4,12,3584]{2,1,0:T(8,128)(2,1)S(1)} async-done(((bf16[4,12,3584]{2,1,0:T(8,128)(2,1)}), bf16[4,12,3584]{2,1,0:T(8,128)(2,1)S(1)}, u32[]{:S(2)}, u32[]{:S(2)}) %all-to-all-start.2) | async-done | bytes 344096 | tf_op jit(solution)/shard_map/all_to_all | solution.py:111
  186.1 0.7 convolution_bitcast_fusion
  186.8 3.9 %fusion.5 = bf16[16,3584]{1,0:T(8,128)(2,1)} fusion(f32[16,3584]{1,0:T(8,128)S(1)} %convolution_bitcast_fusion, bf16[256,3584]{1,0:T(8,128)(2,1)} %param.27, bf16[2,3584,256]{2,1,0:T(8,128)(2,1)} %param.26, bf16[1,16,3584]{2,1,0:T(8,128)(2,1)S(1)} %copy.54, f32[16,256]{1,0:T(8,128)S(1)} %fusion.22), kind=kOutput, calls=%fused_computation.7 | convolution fusion | flops 58859520 | bytes 4145152 | tf_op jit(solution)/shard_map/dot_general | solution.py:125
  190.7 0.0 all-reduce.7.cloned.1.call-update
  190.7 0.0 copy-done.7
  190.7 0.6 dynamic-slice.2
  191.9 33.3 %all-reduce.7.cloned.1.call-done = bf16[16,3584]{1,0:T(8,128)(2,1)} async-done(((bf16[16,3584]{1,0:T(8,128)(2,1)}), bf16[16,3584]{1,0:T(8,128)(2,1)}) %all-reduce.7.cloned.1.call-update) | async-done | bytes 114704
  225.2 2.1 fusion.70
  (21 shorter events, 0.2 us)
Async XLA Ops:
  6.5 1.7 copy-start
  6.5 4.8 %copy-start.1 = (bf16[1,4,128,576]{2,3,1,0:T(8,128)(2,1)S(1)}, bf16[1,4,128,576]{2,3,1,0:T(8,128)(2,1)}, u32[]{:S(2)}) copy-start(bf16[1,4,128,576]{2,3,1,0:T(8,128)(2,1)} %param.15) | copy-start | bytes 1769476
  6.5 4.8 %copy-start.3 = (bf16[1,4,576]{2,1,0:T(4,128)(2,1)S(1)}, bf16[1,4,576]{2,1,0:T(4,128)(2,1)}, u32[]{:S(2)}) copy-start(bf16[1,4,576]{2,1,0:T(4,128)(2,1)} %param.17) | copy-start | bytes 13828
  6.5 129.7 %all-reduce.5.cloned.1.call-start = ((), (), s32[]{:S(2)}) async-start(), calls=%async_computation.3 | async-start | bytes 1835008
  38.0 6.9 %copy-start.4 = (bf16[3584]{0:T(1024)(128)(2,1)S(1)}, bf16[3584]{0:T(1024)(128)(2,1)}, u32[]{:S(2)}) copy-start(bf16[3584]{0:T(1024)(128)(2,1)} %param.22) | copy-start | bytes 21508
  38.0 7.0 %copy-start.5 = (s32[4,4,2]{1,2,0:T(2,128)S(1)}, s32[4,4,2]{1,2,0:T(2,128)}, u32[]{:S(2)}) copy-start(s32[4,4,2]{1,2,0:T(2,128)} %param.19) | copy-start | bytes 388
  38.0 7.3 %copy-start.8 = (u32[32]{0:T(128)S(1)}, u32[32]{0:T(128)}, u32[]{:S(2)}) copy-start(u32[32]{0:T(128)} %constant.40) | copy-start | bytes 388
  38.0 98.3 %copy-start.2 = (bf16[1,4,3584]{2,1,0:T(4,128)(2,1)S(1)}, bf16[1,4,3584]{2,1,0:T(4,128)(2,1)}, u32[]{:S(2)}) copy-start(bf16[1,4,3584]{2,1,0:T(4,128)(2,1)} %param.14) | copy-start | bytes 86020
  43.3 115.0 %copy-start.6 = (bf16[3584,4]{0,1:T(4,128)(2,1)S(1)}, bf16[3584,4]{0,1:T(4,128)(2,1)}, u32[]{:S(2)}) copy-start(bf16[3584,4]{0,1:T(4,128)(2,1)} %param.23) | copy-start | bytes 86020
  154.8 11.6 %all-to-all-start.1 = ((bf16[4,12,3584]{2,1,0:T(8,128)(2,1)}), bf16[4,12,3584]{2,1,0:T(8,128)(2,1)S(1)}, u32[]{:S(2)}, u32[]{:S(2)}) async-start(bf16[4,12,3584]{2,1,0:T(8,128)(2,1)} %convolution_convert_fusion.1), calls=%async_computation.1 | async-start | bytes 917504 | tf_op jit(solution)/shard_map/all_to_all | solution.py:100
  174.6 11.6 %all-to-all-start.2 = ((bf16[4,12,3584]{2,1,0:T(8,128)(2,1)}), bf16[4,12,3584]{2,1,0:T(8,128)(2,1)S(1)}, u32[]{:S(2)}, u32[]{:S(2)}) async-start(bf16[4,12,3584]{2,1,0:T(8,128)(2,1)} %convolution_convert_fusion), calls=%async_computation.2 | async-start | bytes 917504 | tf_op jit(solution)/shard_map/all_to_all | solution.py:111
  178.0 12.7 %copy-start.7 = (u32[32]{0:T(128)S(1)}, u32[32]{0:T(128)}, u32[]{:S(2)}) copy-start(u32[32]{0:T(128)} %constant.44) | copy-start | bytes 388
  178.1 47.2 %all-reduce.7.cloned.1.call-start = ((), (), s32[]{:S(2)}) async-start(), calls=%async_computation.4 | async-start | bytes 229376
Sparse Core Ops, SparseCore 0:
  45.0 91.1 all-reduce.4
  190.8 34.3 all-reduce.6
where the time goes:
time: 235 us; the launch traced here: 234 us
  waiting for transfers between devices  138 us (59%)
  blocking collectives  37.2 us (16%)
  matrix products  26.6 us (11%)
  between operations  15.1 us (6%)
  starting transfers between devices  6.97 us (3%)
  other arithmetic  6.16 us (3%)
  local copies, waits for them, and re-layouts  4.37 us (2%)
    unnamed x4, waiting for transfers between devices  124 us
    all_to_all x1, blocking collectives, on_device(): lax.all_to_all(latent_out, ('ep', 'tp'), split_axis=2, concat_axis=0, til...  22.8 us
    all_gather x1, blocking collectives, on_device(): lax.all_gather(normed.reshape(rows_here * steps_here, model_width), 'tp',...  14.3 us
    all_to_all x1, waiting for transfers between devices, on_device(): lax.all_to_all(outgoing, 'ep', split_axis=0, concat_axis=0, tiled=True)  7.89 us
    all_to_all x1, waiting for transfers between devices, on_device(): lax.all_to_all(produced.astype(jnp.bfloat16), 'ep', split_axis=0, concat_...  6.17 us
    dot_general x1, matrix products, on_device(): jnp.einsum('scf,fd->scd', activated, expert_out[0], preferred_element_typ...  5.4 us
    dot_general x1, matrix products, on_device(): jnp.einsum('rshv,hvd->rsd', head_vals, out_proj, preferred_element_type=j...  5.31 us
  transfers between devices with their start and end apart: 4, of which 4 were waited for; matrix products, arithmetic and copies ran while one was open for 2% of the time, Pallas kernels for 0%

commit v1 on v0

--- a/solution.py
+++ b/solution.py
@@ -61,7 +61,15 @@
     steps_here = hidden_in.shape[1]
     model_width = hidden_in.shape[2]
     latent_out = attend_block(queries, kv_cache, new_kv, lengths)
-    by_head = lax.all_to_all(latent_out, ("ep", "tp"), split_axis=2, concat_axis=0, tiled=True)
+    by_head = jnp.concatenate(
+        lax.all_to_all(
+            jnp.stack(jnp.split(latent_out, lax.axis_size(("ep", "tp")), axis=2)),
+            ("ep", "tp"),
+            0,
+            0,
+        ),
+        axis=0,
+    )
     head_vals = jnp.einsum(
         "rshl,hlv->rshv", by_head, value_up, preferred_element_type=jnp.float32
     ).astype(jnp.bfloat16)

time: 235 us -> 281 us (1.20)
  local copies, waits for them, and re-layouts: 4.37 us -> 48.6 us
    another operation x0 -> x18, local copies, waits for them, and re-layouts: none -> 28 us  [on_device(): jnp.stack(jnp.split(latent_out, lax.axis_size(('ep', 'tp')), axis=2))]
    unnamed x22 -> x37, local copies, waits for them, and re-layouts: 2.08 us -> 18.7 us
  transfers between devices with their start and end apart: 4 -> 4, of which waited for: 4 -> 4; matrix products, arithmetic and copies ran while one was open for 2% -> 1% of each run, Pallas kernels for 0% -> 0%
where the time goes in v1:
time: 281 us; the launch traced here: 279 us
  waiting for transfers between devices  138 us (49%)
  local copies, waits for them, and re-layouts  48.6 us (17%)
  blocking collectives  37.4 us (13%)
  matrix products  26.9 us (10%)
  between operations  15.1 us (5%)
  starting transfers between devices  7.15 us (3%)
  other arithmetic  6.16 us (2%)
    unnamed x4, waiting for transfers between devices  124 us
    another operation x18, local copies, waits for them, and re-layouts, on_device(): jnp.stack(jnp.split(latent_out, lax.axis_size(('ep', 'tp')), axis=2))  28 us
    all_to_all x1, blocking collectives, on_device(): lax.all_to_all(jnp.stack(jnp.split(latent_out, lax.axis_size(('ep', 'tp')...  23 us
    unnamed x37, local copies, waits for them, and re-layouts  18.7 us
    all_gather x1, blocking collectives, on_device(): lax.all_gather(normed.reshape(rows_here * steps_here, model_width), 'tp',...  14.3 us
    all_to_all x1, waiting for transfers between devices, on_device(): lax.all_to_all(outgoing, 'ep', split_axis=0, concat_axis=0, tiled=True)  7.71 us
    all_to_all x1, waiting for transfers between devices, on_device(): lax.all_to_all(produced.astype(jnp.bfloat16), 'ep', split_axis=0, concat_...  6.17 us
  transfers between devices with their start and end apart: 4, of which 4 were waited for; matrix products, arithmetic and copies ran while one was open for 1% of the time, Pallas kernels for 0%

profile of v1, /device:TPU:0, one launch (start us, length us, event | category | flops | bytes accessed | tf_op | source)
XLA Modules:
  0.0 278.8 jit_solution(7044764936408304026)
XLA Ops:
  7.4 0.8 copy-done
  8.2 3.2 %fusion.6 = (f32[4,128]{1,0:T(4,128)S(1)}, f32[4,128,2048]{2,1,0:T(8,128)S(1)}) fusion(pred[2048]{0:T(1024)(128)(4,1)S(1)} %iota_compare_fusion.1, bf16[1,2048,576]{1,2,0:T(8,128)(2,1)S(1)} %copy-done, bf16[1,4,128,576]{2,3,1,0:T(8,128)(2,1)} %param.15), kind=kOutput, calls=%fused_computation.11 | convolution fusion | flops 1211104768 | bytes 7147520 | tf_op jit(solution)/shard_map/rshk,rck->rshc/dot_general | solution.py:16
  11.6 0.9 fusion.14
  12.6 1.7 fusion.15
  14.7 4.0 %slice_bitcast_fusion = (bf16[1,1,4,8,512]{3,4,2,1,0:T(8,128)(2,1)S(1)}, bf16[1,1,4,8,512]{3,4,2,1,0:T(8,128)(2,1)S(1)}, bf16[1,1,4,8,512]{3,4,2,1,0:T(8,128)(2,...) fusion(bf16[1,4,128,576]{2,3,1,0:T(8,128)(2,1)S(1)} %fusion.27), kind=kLoop, calls=%fused_computation.50 | loop fusion | bytes 1048576 | tf_op jit(solution)/shard_map/stack | solution.py:66
  18.7 1.2 copy.54
  20.5 1.8 copy.55
  22.3 1.8 copy.56
  24.2 1.8 copy.57
  26.0 1.8 copy.58
  27.8 1.8 copy.59
  29.6 1.8 copy.60
  31.4 1.8 copy.61
  33.2 1.8 copy.62
  35.0 1.8 copy.63
  36.9 1.8 copy.64
  38.7 1.2 copy.65
  39.9 1.2 copy.66
  41.1 1.2 copy.67
  42.7 1.4 constant_dynamic-update-slice_fusion.14
  44.1 1.4 constant_dynamic-update-slice_fusion.13
  45.4 1.4 constant_dynamic-update-slice_fusion.12
  46.8 1.4 constant_dynamic-update-slice_fusion.11
  48.1 1.4 constant_dynamic-update-slice_fusion.10
  49.5 1.4 constant_dynamic-update-slice_fusion.9
  50.9 1.4 constant_dynamic-update-slice_fusion.8
  52.2 1.4 constant_dynamic-update-slice_fusion.7
  53.6 1.4 constant_dynamic-update-slice_fusion.6
  55.0 1.4 constant_dynamic-update-slice_fusion.5
  59.3 23.0 %all_to_all.15 = bf16[16,1,4,8,512]{4,3,2,1,0:T(8,128)(2,1)} all-to-all(bf16[16,1,4,8,512]{4,3,2,1,0:T(8,128)(2,1)} %constant_dynamic-update-slice_fusion), channel_id=1, replica_groups=mesh['groups'=2,'ep'=4,'tp'=4] {'ep','tp'}, dimensions={0} | all-to-all | bytes 1048576 | tf_op jit(solution)/shard_map/all_to_all | solution.py:65
  82.4 5.6 %fusion.2 = f32[16,4,3584]{2,0,1:T(8,128)S(1)} fusion(bf16[8,128,3584]{2,1,0:T(8,128)(2,1)} %param.21, bf16[8,512,128]{2,1,0:T(8,128)(2,1)} %param.20, bf16[16,1,4,8,512]{4,3,2,1,0:T(8,128)(2,1)} %all_to_all.15), kind=kOutput, calls=%fused_computation.2 | convolution fusion | flops 536936448 | bytes 9830400 | tf_op jit(solution)/shard_map/rshv,hvd->rsd/dot_general | solution.py:77
  88.0 1.6 copy.71
  90.6 90.4 %all-reduce.5.cloned.1.call-done = f32[16,4,3584]{2,1,0:T(4,128)} async-done(((f32[16,4,3584]{2,1,0:T(4,128)}), f32[16,4,3584]{2,1,0:T(4,128)}) %all-reduce.5.cloned.1.call-update) | async-done | bytes 917520
  180.9 1.5 multiply_reduce_fusion
  182.5 1.5 multiply_convert_fusion
  184.0 14.3 %all-gather = bf16[1,16,3584]{2,0,1:T(2,128)(2,1)S(1)} all-gather(bf16[1,4,3584]{2,0,1:T(2,128)(2,1)S(1)} %copy.76), channel_id=2, replica_groups=mesh['groups'=2,'ep'=4,'tp'=4] {'tp'}, dimensions={1}, use_global_device_ids=true | all-gather | bytes 143360 | tf_op jit(solution)/shard_map/all_gather | solution.py:87
  198.4 1.2 convolution_convert_fusion.1
  199.5 3.6 %all-to-all-start.1 = ((bf16[4,12,3584]{2,1,0:T(8,128)(2,1)}), bf16[4,12,3584]{2,1,0:T(8,128)(2,1)S(1)}, u32[]{:S(2)}, u32[]{:S(2)}) async-start(bf16[4,12,3584]{2,1,0:T(8,128)(2,1)} %convolution_convert_fusion.1), calls=%async_computation.1 | async-start | bytes 917504 | tf_op jit(solution)/shard_map/all_to_all | solution.py:108
  203.4 7.7 %all-to-all-done.1 = bf16[4,12,3584]{2,1,0:T(8,128)(2,1)S(1)} async-done(((bf16[4,12,3584]{2,1,0:T(8,128)(2,1)}), bf16[4,12,3584]{2,1,0:T(8,128)(2,1)S(1)}, u32[]{:S(2)}, u32[]{:S(2)}) %all-to-all-start.1) | async-done | bytes 344096 | tf_op jit(solution)/shard_map/all_to_all | solution.py:108
  211.1 2.8 fusion.9
  213.9 5.4 %convolution_convert_fusion = bf16[4,12,3584]{2,1,0:T(8,128)(2,1)} fusion(bf16[1,512,3584]{2,1,0:T(8,128)(2,1)} %param.25, bf16[4,12,3584]{2,1,0:T(8,128)(2,1)S(1)} %all-to-all-done.1, bf16[1,2,3584,512]{3,2,1,0:T(8,128)(2,1)} %param.24, f32[4,12,512]{2,1,0:T(8,128)S(1)} %fusion.9), kind=kOutput, calls=%fused_computation.3 | convolution fusion | flops 352641024 | bytes 8126464 | tf_op jit(solution)/shard_map/scf,fd->scd/dot_general | solution.py:116
  219.3 3.5 %all-to-all-start.2 = ((bf16[4,12,3584]{2,1,0:T(8,128)(2,1)}), bf16[4,12,3584]{2,1,0:T(8,128)(2,1)S(1)}, u32[]{:S(2)}, u32[]{:S(2)}) async-start(bf16[4,12,3584]{2,1,0:T(8,128)(2,1)} %convolution_convert_fusion), calls=%async_computation.2 | async-start | bytes 917504 | tf_op jit(solution)/shard_map/all_to_all | solution.py:119
  222.8 1.8 fusion.22
  224.6 6.2 %all-to-all-done.2 = bf16[4,12,3584]{2,1,0:T(8,128)(2,1)S(1)} async-done(((bf16[4,12,3584]{2,1,0:T(8,128)(2,1)}), bf16[4,12,3584]{2,1,0:T(8,128)(2,1)S(1)}, u32[]{:S(2)}, u32[]{:S(2)}) %all-to-all-start.2) | async-done | bytes 344096 | tf_op jit(solution)/shard_map/all_to_all | solution.py:119
  230.8 0.7 convolution_bitcast_fusion
  231.5 3.9 %fusion.5 = bf16[16,3584]{1,0:T(8,128)(2,1)} fusion(f32[16,3584]{1,0:T(8,128)S(1)} %convolution_bitcast_fusion, bf16[256,3584]{1,0:T(8,128)(2,1)} %param.27, bf16[2,3584,256]{2,1,0:T(8,128)(2,1)} %param.26, bf16[1,16,3584]{2,1,0:T(8,128)(2,1)S(1)} %copy.81, f32[16,256]{1,0:T(8,128)S(1)} %fusion.22), kind=kOutput, calls=%fused_computation.7 | convolution fusion | flops 58859520 | bytes 4145152 | tf_op jit(solution)/shard_map/dot_general | solution.py:133
  236.6 33.3 %all-reduce.7.cloned.1.call-done = bf16[16,3584]{1,0:T(8,128)(2,1)} async-done(((bf16[16,3584]{1,0:T(8,128)(2,1)}), bf16[16,3584]{1,0:T(8,128)(2,1)}) %all-reduce.7.cloned.1.call-update) | async-done | bytes 114704
  269.9 2.1 fusion.69
  (52 shorter events, 6.5 us)
Async XLA Ops:
  6.5 1.7 copy-start
  6.5 4.8 %copy-start.1 = (bf16[1,4,128,576]{2,3,1,0:T(8,128)(2,1)S(1)}, bf16[1,4,128,576]{2,3,1,0:T(8,128)(2,1)}, u32[]{:S(2)}) copy-start(bf16[1,4,128,576]{2,3,1,0:T(8,128)(2,1)} %param.15) | copy-start | bytes 1769476
  6.5 4.8 %copy-start.3 = (bf16[1,4,576]{2,1,0:T(4,128)(2,1)S(1)}, bf16[1,4,576]{2,1,0:T(4,128)(2,1)}, u32[]{:S(2)}) copy-start(bf16[1,4,576]{2,1,0:T(4,128)(2,1)} %param.17) | copy-start | bytes 13828
  6.5 174.4 %all-reduce.5.cloned.1.call-start = ((), (), s32[]{:S(2)}) async-start(), calls=%async_computation.3 | async-start | bytes 1835008
  82.4 7.2 %copy-start.4 = (bf16[3584]{0:T(1024)(128)(2,1)S(1)}, bf16[3584]{0:T(1024)(128)(2,1)}, u32[]{:S(2)}) copy-start(bf16[3584]{0:T(1024)(128)(2,1)} %param.22) | copy-start | bytes 21508
  82.4 7.2 %copy-start.5 = (s32[4,4,2]{1,2,0:T(2,128)S(1)}, s32[4,4,2]{1,2,0:T(2,128)}, u32[]{:S(2)}) copy-start(s32[4,4,2]{1,2,0:T(2,128)} %param.19) | copy-start | bytes 388
  82.4 7.6 %copy-start.8 = (u32[32]{0:T(128)S(1)}, u32[32]{0:T(128)}, u32[]{:S(2)}) copy-start(u32[32]{0:T(128)} %constant.40) | copy-start | bytes 388
  82.4 98.5 %copy-start.2 = (bf16[1,4,3584]{2,1,0:T(4,128)(2,1)S(1)}, bf16[1,4,3584]{2,1,0:T(4,128)(2,1)}, u32[]{:S(2)}) copy-start(bf16[1,4,3584]{2,1,0:T(4,128)(2,1)} %param.14) | copy-start | bytes 86020
  88.0 115.2 %copy-start.6 = (bf16[3584,4]{0,1:T(4,128)(2,1)S(1)}, bf16[3584,4]{0,1:T(4,128)(2,1)}, u32[]{:S(2)}) copy-start(bf16[3584,4]{0,1:T(4,128)(2,1)} %param.23) | copy-start | bytes 86020
  199.5 11.6 %all-to-all-start.1 = ((bf16[4,12,3584]{2,1,0:T(8,128)(2,1)}), bf16[4,12,3584]{2,1,0:T(8,128)(2,1)S(1)}, u32[]{:S(2)}, u32[]{:S(2)}) async-start(bf16[4,12,3584]{2,1,0:T(8,128)(2,1)} %convolution_convert_fusion.1), calls=%async_computation.1 | async-start | bytes 917504 | tf_op jit(solution)/shard_map/all_to_all | solution.py:108
  219.3 11.6 %all-to-all-start.2 = ((bf16[4,12,3584]{2,1,0:T(8,128)(2,1)}), bf16[4,12,3584]{2,1,0:T(8,128)(2,1)S(1)}, u32[]{:S(2)}, u32[]{:S(2)}) async-start(bf16[4,12,3584]{2,1,0:T(8,128)(2,1)} %convolution_convert_fusion), calls=%async_computation.2 | async-start | bytes 917504 | tf_op jit(solution)/shard_map/all_to_all | solution.py:119
  222.7 12.7 %copy-start.7 = (u32[32]{0:T(128)S(1)}, u32[32]{0:T(128)}, u32[]{:S(2)}) copy-start(u32[32]{0:T(128)} %constant.44) | copy-start | bytes 388
  222.8 47.1 %all-reduce.7.cloned.1.call-start = ((), (), s32[]{:S(2)}) async-start(), calls=%async_computation.4 | async-start | bytes 229376
Sparse Core Ops, SparseCore 0:
  89.7 91.1 all-reduce.4
  235.5 34.3 all-reduce.6
